TPU v7x, 32 devices: a whole 2x2x4 slice. The times are simulated.
32 devices in a mesh: groups: 2 (over y), row: 16 (over z, x, core).
Axes of the slice: x: 2, y: 2, z: 4, core: 2. Of those that a mesh axis runs over, the one named last changes fastest.
Arguments:
- raw_samples: bfloat16 [8, 1536, 1280], P('groups', 'row'), parts along dimension 0, may hold values from -64 to 64, as said below
- partner: int32 [32, 3], P(('groups', 'row')), parts along dimension 0, may hold values from -1 to 15, as said below
- counts: int32 [32, 3], P(('groups', 'row')), parts along dimension 0, may hold values from 1 to 4
Outputs:
- correlations: bfloat16 [32, 3, 80, 80, 128], P(('groups', 'row')), parts along dimension 0
There are 2 independent parts, one for each index of `groups`. A program takes and returns all parts, laid end to end along the dimension named above; each array names one. Nothing has to cross between parts.
Inputs may be any that keep to these rules, and one draw needn't show every extreme that they name: `raw_samples`: strain values of each channel and segment at their own scale. `partner`: slot 0 of row i holds i; slots 1 to r hold i + 1 to i + r for some r of 0 to 2 with i + r < 16; the other slots hold -1. Some row has r = 2. A tile stacks its first counts segments.
All inputs are finite; a program needn't handle non-finite values.
Results may differ from a plain program's by a relative error of at most 0.0075.
Values may be sent and summed in bfloat16 or wider, within the bound.
A program may use at most 128 MiB of HBM per device.

v0:
```python
import functools
import math

import jax
import jax.numpy as jnp
import numpy as np
from jax import lax
from jax.experimental import pallas as pl
from jax.experimental.pallas import tpu as pltpu
from jax.sharding import PartitionSpec as P

SAMPLES = 1536
BINS = 192
FIRST_BIN = 5
LAGS = 128
LAG_STEP = 4
SLOTS = 3
WIDTH = 2 * BINS
HALF = BINS - 128
ROWS_PER_STEP = 16
MESH = pl.DeviceIdType.MESH


def bin_order():
    bins = np.concatenate([np.arange(BINS), np.arange(128, BINS), np.arange(128)])
    imag = np.arange(WIDTH) >= BINS
    return bins, imag


def angle(product):
    return np.float32(2.0 * math.pi / SAMPLES) * (product % SAMPLES).astype(np.float32)


def forward_table():
    bins, imag = bin_order()
    angles = angle(np.arange(SAMPLES)[:, None] * (FIRST_BIN + bins)[None, :])
    return jnp.asarray(np.where(imag[None, :], -np.sin(angles), np.cos(angles)).astype(np.float32)).astype(jnp.bfloat16)


def lag_tables():
    bins, imag = bin_order()
    delays = LAG_STEP * (np.arange(LAGS) - LAGS // 2)
    angles = angle(delays[:, None] * (FIRST_BIN + bins)[None, :])
    straight = np.cos(angles).astype(np.float32)
    crossed = np.where(imag[None, :], -np.sin(angles), np.sin(angles)).astype(np.float32)
    return jnp.asarray(straight).astype(jnp.bfloat16), jnp.asarray(crossed).astype(jnp.bfloat16)


def spectra_kernel(n, segments, raw, table, own, near, far, turned, landed, acc, send_sem, recv_sem, pass_send, pass_recv):
    me = lax.axis_index("row")
    block = own.shape[1]
    local = table.shape[1]
    barrier = pltpu.get_barrier_semaphore()

    def ahead(k):
        return lax.rem(me + k, n)

    @pl.loop(1, n)
    def _(k):
        pl.semaphore_signal(barrier, inc=1, device_id={"row": ahead(k)}, device_id_type=MESH)

    @pl.loop(0, raw.shape[1] // 128)
    def _(i):
        part = pl.ds(pl.multiple_of(i * 128, 128), 128)
        turned[part, :] = raw[:, part].T

    pl.semaphore_wait(barrier, n - 1)

    def block_copy(k):
        target = ahead(k)
        return pltpu.make_async_remote_copy(
            src_ref=turned.at[pl.ds(pl.multiple_of(target * block, 16), block)],
            dst_ref=landed.at[me],
            send_sem=send_sem.at[k],
            recv_sem=recv_sem.at[k],
            device_id={"row": target},
            device_id_type=MESH,
        )

    @pl.loop(1, n)
    def _(k):
        block_copy(k).start()

    def transform(x, source):
        stacked = jnp.concatenate([x[:, s * local:(s + 1) * local] for s in range(segments)], axis=0)
        return jnp.dot(stacked, table[source], preferred_element_type=jnp.float32)

    acc[...] = transform(turned[pl.ds(pl.multiple_of(me * block, 16), block), :], me)

    @pl.loop(1, n)
    def _(k):
        block_copy(k).wait_recv()
        source = lax.rem(me + n - k, n)
        acc[...] += transform(landed[source], source)

    spectra = acc[...]
    energy = 2.0 * jnp.mean(spectra * spectra, axis=-1, keepdims=True)
    white = (spectra * lax.rsqrt(energy + 1e-06)).astype(jnp.bfloat16)
    for s in range(segments):
        own[s] = white[s * block:(s + 1) * block]

    def pass_copy(i, target, place):
        return pltpu.make_async_remote_copy(
            src_ref=own, dst_ref=place, send_sem=pass_send.at[i], recv_sem=pass_recv.at[i],
            device_id={"row": target}, device_id_type=MESH,
        )

    for i, place in enumerate((near, far)):
        @pl.when(me >= i + 1)
        def _():
            pass_copy(i, lax.rem(me + n - i - 1, n), place).start()

        @pl.when(me + i + 1 >= n)
        def _():
            place[...] = jnp.zeros_like(place)

    @pl.loop(1, n)
    def _(k):
        block_copy(k).wait_send()

    for i, place in enumerate((near, far)):
        @pl.when(me + i + 1 < n)
        def _():
            pass_copy(i, lax.rem(me + n - i - 1, n), place).wait_recv()

        @pl.when(me >= i + 1)
        def _():
            pass_copy(i, lax.rem(me + n - i - 1, n), place).wait_send()


def white_blocks(raw_samples):
    n = lax.axis_size("row")
    segments, local, channels = raw_samples.shape
    block = channels // n
    white = jax.ShapeDtypeStruct((segments, block, WIDTH), jnp.bfloat16)
    vmem = pl.BlockSpec(memory_space=pltpu.VMEM)
    return pl.pallas_call(
        functools.partial(spectra_kernel, n, segments),
        out_shape=(white,) * 3,
        in_specs=[vmem] * 2,
        out_specs=(vmem,) * 3,
        scratch_shapes=[
            pltpu.VMEM((channels, segments * local), jnp.bfloat16),
            pltpu.VMEM((n, block, segments * local), jnp.bfloat16),
            pltpu.VMEM((segments * block, WIDTH), jnp.float32),
            pltpu.SemaphoreType.DMA((n,)),
            pltpu.SemaphoreType.DMA((n,)),
            pltpu.SemaphoreType.DMA((2,)),
            pltpu.SemaphoreType.DMA((2,)),
        ],
        compiler_params=pltpu.CompilerParams(collective_id=0, has_side_effects=True, vmem_limit_bytes=25000000),
        cost_estimate=pl.CostEstimate(flops=20_000_000_000, bytes_accessed=4_000_000, transcendentals=0),
        name="white_blocks",
    )(raw_samples.reshape(segments * local, channels), forward_table().reshape(n, local, WIDTH))


def correlate_kernel(partner, counts, own, near, far, t1, t2, out, right, rows, swapped, w0, w1):
    segments, block, width = own.shape
    step = pl.program_id(0)

    @pl.when(step == 0)
    def _():
        for slot, source in enumerate((own, near, far)):
            seg_count = counts[0, slot]
            for s in range(segments):
                keep = (s < seg_count).astype(jnp.float32)
                right[slot * block:(slot + 1) * block, s * width:(s + 1) * width] = (
                    source[s].astype(jnp.float32) * keep).astype(jnp.bfloat16)
        for s in range(segments):
            value = own[s].astype(jnp.float32)
            rows[s] = value
            swapped[s, :, 0:128] = value[:, 256:384]
            swapped[s, :, 256:384] = value[:, 0:128]
            swapped[s, :, 128:256] = pltpu.roll(value[:, 128:256], HALF, 1)

    buffers = (w0, w1)
    first = pl.multiple_of(step * ROWS_PER_STEP, ROWS_PER_STEP)
    scales = []
    for slot in range(SLOTS):
        live = (partner[0, slot] >= 0).astype(jnp.float32)
        count = jnp.full((8, LAGS), counts[0, slot].astype(jnp.float32), jnp.float32)
        scales.append((lax.rsqrt(count) * (live * (1.0 / math.sqrt(BINS))))[0:1])

    def fill(pair, base):
        w = buffers[pair % 2]
        for s in range(segments):
            x8 = rows[s, pl.ds(base, ROWS_PER_STEP), :]
            y8 = swapped[s, pl.ds(base, ROWS_PER_STEP), :]
            for k in range(2):
                i = 2 * pair + k
                x = jnp.broadcast_to(x8[i:i + 1], (16, width)).astype(jnp.bfloat16)
                y = jnp.broadcast_to(y8[i:i + 1], (16, width)).astype(jnp.bfloat16)
                for m in range(0, LAGS, 16):
                    w[k * LAGS + m:k * LAGS + m + 16, s * width:(s + 1) * width] = (
                        x * t1[m:m + 16, :] + y * t2[m:m + 16, :])

    pairs = ROWS_PER_STEP // 2
    later = pl.multiple_of(jnp.minimum(first + ROWS_PER_STEP, block - ROWS_PER_STEP), ROWS_PER_STEP)

    @pl.when(step == 0)
    def _():
        fill(0, first)

    for pair in range(pairs):
        if pair + 1 < pairs:
            fill(pair + 1, first)
        else:
            fill(0, later)
        result = lax.dot_general(right[...], buffers[pair % 2][...], (((1,), (1,)), ((), ())),
                                 preferred_element_type=jnp.float32)
        for k in range(2):
            a = first + 2 * pair + k
            part = result[:, k * LAGS:(k + 1) * LAGS]
            for slot in range(SLOTS):
                tile = part[slot * block:(slot + 1) * block] * scales[slot]
                if slot == 0:
                    tile = jnp.where(lax.broadcasted_iota(jnp.int32, tile.shape, 0) > a, tile, 0.0)
                out[0, slot, 2 * pair + k] = tile.astype(jnp.bfloat16)


def correlate(partner, counts, own, near, far):
    segments, block, width = own.shape
    t1, t2 = lag_tables()
    vmem = pl.BlockSpec(memory_space=pltpu.VMEM)
    depth = segments * width
    return pl.pallas_call(
        correlate_kernel,
        grid_spec=pltpu.PrefetchScalarGridSpec(
            num_scalar_prefetch=0,
            grid=(block // ROWS_PER_STEP,),
            in_specs=[pl.BlockSpec(memory_space=pltpu.SMEM)] * 2 + [vmem] * 5,
            out_specs=pl.BlockSpec((1, SLOTS, ROWS_PER_STEP, block, LAGS), lambda i, *_: (0, 0, i, 0, 0)),
            scratch_shapes=[
                pltpu.VMEM((SLOTS * block, depth), jnp.bfloat16),
                pltpu.VMEM(own.shape, jnp.float32),
                pltpu.VMEM(own.shape, jnp.float32),
                pltpu.VMEM((2 * LAGS, depth), jnp.bfloat16),
                pltpu.VMEM((2 * LAGS, depth), jnp.bfloat16),
            ],
        ),
        out_shape=jax.ShapeDtypeStruct((1, SLOTS, block, block, LAGS), jnp.bfloat16),
        cost_estimate=pl.CostEstimate(flops=2 * SLOTS * block * block * LAGS * depth, bytes_accessed=6_000_000, transcendentals=0),
        compiler_params=pltpu.CompilerParams(vmem_limit_bytes=20 * 2**20),
        name="correlate",
    )(partner, counts, own, near, far, t1, t2)


def on_device(raw_samples, partner, counts):
    own, near, far = white_blocks(raw_samples)
    return correlate(partner, counts, own, near, far)


def solution(mesh):
    return jax.shard_map(
        on_device,
        mesh=mesh,
        in_specs=(P("groups", "row", None), P(("groups", "row"), None), P(("groups", "row"), None)),
        out_specs=P(("groups", "row"), None, None, None, None),
        check_vma=False,
    )
```

profile of v0, /device:TPU:24, one launch (start us, length us, event | category | flops | bytes accessed | tf_op | source)
XLA Modules:
  0.0 54.1 jit_solution(4800698359509024007)
XLA Ops:
  0.0 0.0 copy-start
  0.0 1.2 %copy-done = bf16[4,96,1280]{2,1,0:T(8,128)(2,1)S(1)} copy-done((bf16[4,96,1280]{2,1,0:T(8,128)(2,1)S(1)}, bf16[4,96,1280]{2,1,0:T(8,128)(2,1)}, u32[]{:S(2)}) %copy-start) | copy-done | bytes 983064
  1.2 0.0 copy-start.3
  1.2 1.3 %copy-done.3 = bf16[16,96,384]{2,1,0:T(8,128)(2,1)S(1)} copy-done((bf16[16,96,384]{2,1,0:T(8,128)(2,1)S(1)}, bf16[16,96,384]{2,1,0:T(8,128)(2,1)}, u32[]{:S(2)}) %copy-start.3) | copy-done | bytes 1179672
  2.5 0.0 copy-start.1
  2.5 0.0 copy-start.2
  2.5 0.0 copy-start.4
  2.5 0.0 copy-start.5
  2.5 37.9 %white_blocks.1 = (bf16[4,80,384]{2,1,0:T(8,128)(2,1)S(1)}, bf16[4,80,384]{2,1,0:T(8,128)(2,1)S(1)}, bf16[4,80,384]{2,1,0:T(8,128)(2,1)S(1)}) custom-call(bf16[384,1280]{1,0:T(8,128)(2,1)S(1)} %bitcast.1, bf16[16,96,384]{2,1,0:T(8,128)(2,1)S(1)} %copy-done.3), custom_call_target="tpu_custom_call" | custom-call | flops 20000000000 | bytes 4000000 | tf_op jit(solution)/shard_map/white_blocks/pallas_call | solution.py:137
  40.4 0.0 copy-done.1
  40.4 0.0 copy-done.2
  40.4 0.0 copy-done.4
  40.4 0.0 copy-done.5
  40.4 13.7 %correlate.1 = bf16[1,3,80,80,128]{4,3,2,1,0:T(8,128)(2,1)} custom-call(s32[1,3]{1,0:T(1,128)S(1)} %copy-done.1, s32[1,3]{1,0:T(1,128)S(1)} %copy-done.2, bf16[4,80,384]{2,1,0:T(8,128)(2,1)S(1)} %get-tuple-element.8.own, bf16[4,80,384]{2,1,0:T(8,128)(2,1)S(1)} %get-tuple-element.9.near, bf16[4,80,384]{2,1,0:T(8,128)(2,1)S(1)} %get-tuple-element.10.far, ...), custom_call_target="tpu_custom_call" | custom-call | flops 7549747200 | bytes 6000000 | tf_op jit(solution)/shard_map/correlate/pallas_call | solution.py:226
Async XLA Ops:
  0.0 1.2 %copy-start = (bf16[4,96,1280]{2,1,0:T(8,128)(2,1)S(1)}, bf16[4,96,1280]{2,1,0:T(8,128)(2,1)}, u32[]{:S(2)}) copy-start(bf16[4,96,1280]{2,1,0:T(8,128)(2,1)} %param.6) | copy-start | bytes 2949124
  1.2 1.3 %copy-start.3 = (bf16[16,96,384]{2,1,0:T(8,128)(2,1)S(1)}, bf16[16,96,384]{2,1,0:T(8,128)(2,1)}, u32[]{:S(2)}) copy-start(bf16[16,96,384]{2,1,0:T(8,128)(2,1)} %constant.12.table) | copy-start | bytes 3538948
  2.5 37.9 %copy-start.1 = (s32[1,3]{1,0:T(1,128)S(1)}, s32[1,3]{1,0:T(1,128)}, u32[]{:S(2)}) copy-start(s32[1,3]{1,0:T(1,128)} %partner.1) | copy-start | bytes 40
  2.5 37.9 %copy-start.2 = (s32[1,3]{1,0:T(1,128)S(1)}, s32[1,3]{1,0:T(1,128)}, u32[]{:S(2)}) copy-start(s32[1,3]{1,0:T(1,128)} %counts.1) | copy-start | bytes 40
  2.5 37.9 %copy-start.4 = (bf16[128,384]{1,0:T(8,128)(2,1)S(1)}, bf16[128,384]{1,0:T(8,128)(2,1)}, u32[]{:S(2)}) copy-start(bf16[128,384]{1,0:T(8,128)(2,1)} %constant.14.t2) | copy-start | bytes 294916
  2.5 37.9 %copy-start.5 = (bf16[128,384]{1,0:T(8,128)(2,1)S(1)}, bf16[128,384]{1,0:T(8,128)(2,1)}, u32[]{:S(2)}) copy-start(bf16[128,384]{1,0:T(8,128)(2,1)} %constant.13.t1) | copy-start | bytes 294916
where the time goes:
time: 54.3 us; the launch traced here: 54.1 us
  Pallas kernels  51.6 us (95%)
  local copies, waits for them, and re-layouts  2.49 us (5%)
    pallas_call x1, Pallas kernels, white_blocks(): pl.pallas_call(functools.partial(spectra_kernel, n, segments), out_shape=...  37.9 us
    pallas_call x1, Pallas kernels, correlate(): pl.pallas_call(correlate_kernel, grid_spec=pltpu.PrefetchScalarGridSpec(n...  13.7 us
    unnamed x12, local copies, waits for them, and re-layouts  2.49 us

commit v1 on v0

v1 whole, which is shorter than its diff:
```python
import functools
import math

import jax
import jax.numpy as jnp
import numpy as np
from jax import lax
from jax.experimental import pallas as pl
from jax.experimental.pallas import tpu as pltpu
from jax.sharding import PartitionSpec as P

SAMPLES = 1536
BINS = 192
FIRST_BIN = 5
LAGS = 128
LAG_STEP = 4
SLOTS = 3
WIDTH = 2 * BINS
HALF = BINS - 128
PARTS = WIDTH // 128
GROUP = 8
ROWS_PER_STEP = 16
MESH = pl.DeviceIdType.MESH


def bin_order():
    bins = np.concatenate([np.arange(BINS), np.arange(128, BINS), np.arange(128)])
    imag = np.arange(WIDTH) >= BINS
    return bins, imag


def angle(product):
    return np.float32(2.0 * math.pi / SAMPLES) * (product % SAMPLES).astype(np.float32)


def forward_table():
    bins, imag = bin_order()
    angles = angle(np.arange(SAMPLES)[:, None] * (FIRST_BIN + bins)[None, :])
    return jnp.asarray(np.where(imag[None, :], -np.sin(angles), np.cos(angles)).astype(np.float32)).astype(jnp.bfloat16)


def lag_tables():
    bins, imag = bin_order()
    delays = LAG_STEP * (np.arange(LAGS) - LAGS // 2)
    angles = angle(delays[:, None] * (FIRST_BIN + bins[:256])[None, :])
    straight = np.cos(angles).astype(np.float32)
    crossed = np.where(imag[None, :256], -np.sin(angles), np.sin(angles)).astype(np.float32)
    tables = np.stack([straight[:, :128], straight[:, 128:], crossed[:, :128], crossed[:, 128:]])
    return jnp.asarray(tables).astype(jnp.bfloat16)


def tile_plan(segments, local):
    lanes = segments * local
    width = 128 if lanes % 128 == 0 else lanes
    tiles = lanes // width
    parts = [(s, t) for s in range(segments) for t in range(PARTS)]
    pieces, stages, done, used = [], [], 0, 0
    for j in range(tiles):
        row = []
        for s in range(segments):
            lo, hi = max(s * local, j * width), min((s + 1) * local, (j + 1) * width)
            if lo < hi:
                row.append((s, lo - j * width, hi - j * width, lo - s * local))
        pieces.append(row)
        whole = (j + 1) * width // local
        if whole > done:
            ready = whole * PARTS
            ready -= ready % 2 if j < tiles - 1 else 0
            stages.append((j, list(range(done, whole)), parts[used:ready]))
            done, used = whole, ready
    return width, pieces, stages


def turned_pair(rows, mid, lag, parts, base, first):
    halves = []
    for k in range(2):
        i = first + k
        columns = []
        for s, t in parts:
            if t == 1:
                x, y, c = rows[s, 1, pl.ds(base, GROUP), :], mid[s, pl.ds(base, GROUP), :], 1
            else:
                x, y, c = rows[s, t, pl.ds(base, GROUP), :], rows[s, 2 - t, pl.ds(base, GROUP), :], 0
            x, y = (jnp.broadcast_to(v[i:i + 1], (16, 128)).astype(jnp.bfloat16) for v in (x, y))
            column = []
            for m in range(0, LAGS, 16):
                straight, crossed = x * lag[c, m:m + 16], y * lag[c + 2, m:m + 16]
                column.append(straight - crossed if t == 2 else straight + crossed)
            columns.append(jnp.concatenate(column, axis=0))
        halves.append(jnp.concatenate(columns, axis=1))
    return jnp.concatenate(halves, axis=0)


def turn_rows(rows, mid, s, value):
    for t in range(PARTS):
        rows[s, t] = value[:, t * 128:(t + 1) * 128]
    mid[s] = pltpu.roll(value[:, 128:256], HALF, 1)


def lag_dot(right, turned, parts):
    left = jnp.concatenate([right[t] for t in range(parts)], axis=1)
    return lax.dot_general(left, turned, (((1,), (1,)), ((), ())), preferred_element_type=jnp.float32)


def slot_scale(partner, counts, slot):
    live = (partner[0, slot] >= 0).astype(jnp.float32)
    count = jnp.full((8, LAGS), counts[0, slot].astype(jnp.float32), jnp.float32)
    return (lax.rsqrt(count) * (live * (1.0 / math.sqrt(BINS))))[0:1]


def masked(source, s, t, counts, slot):
    return (source[s, t].astype(jnp.float32) * (s < counts[0, slot]).astype(jnp.float32)).astype(jnp.bfloat16)


def exchange_kernel(n, width, pieces, stages, raw, table_hbm, lag_hbm, counts_hbm, own, near, far, acc,
                    raw_v, table, lag, counts, turned, landed, spec, right, rows, mid, load_sem, send_sem, recv_sem, pass_send, pass_recv):
    me = lax.axis_index("row")
    segments, _, block, _ = own.shape
    tiles = len(pieces)
    channels = turned.shape[1]
    barrier = pltpu.get_barrier_semaphore()

    def ahead(k):
        return lax.rem(me + k, n)

    @pl.loop(1, n)
    def _(k):
        pl.semaphore_signal(barrier, inc=1, device_id={"row": ahead(k)}, device_id_type=MESH)

    loads = [pltpu.make_async_copy(raw.at[j], raw_v.at[j], load_sem.at[j]) for j in range(tiles)]
    more = [pltpu.make_async_copy(source, place, load_sem.at[tiles + i]) for i, (source, place) in enumerate(
        ((counts_hbm, counts), (table_hbm, table), (lag_hbm, lag)))]
    for copy in loads + more:
        copy.start()

    def tile_copy(j, k):
        target = ahead(k)
        return pltpu.make_async_remote_copy(
            src_ref=turned.at[j, pl.ds(pl.multiple_of(target * block, 16), block)],
            dst_ref=landed.at[j, me],
            send_sem=send_sem.at[j, k],
            recv_sem=recv_sem.at[j, k],
            device_id={"row": target},
            device_id_type=MESH,
        )

    def send(j, lo, hi):
        @pl.loop(lo, hi)
        def _(k):
            tile_copy(j, k).start()

    half = n // 2

    def send_next(j):
        if tiles > 2 and j < 2:
            for i in range(2, tiles):
                send(i, *((1, half), (half, n))[j])

    for j in range(tiles):
        loads[j].wait()

        @pl.loop(0, channels // 128)
        def _(i):
            part = pl.ds(pl.multiple_of(i * 128, 128), 128)
            turned[j, part, :] = raw_v[j, :, part].T

        if j == 0:
            pl.semaphore_wait(barrier, n - 1)
        if j < 2:
            send(j, 1, n)

    for copy in more:
        copy.wait()

    def transform(j, source, x, fresh):
        for s, lo, hi, t in pieces[j]:
            part = jnp.dot(x[:, lo:hi], table[source, t:t + hi - lo], preferred_element_type=jnp.float32)
            spec[s] = part if fresh and t == 0 else spec[s] + part

    def spectra_first(j):
        transform(j, me, turned[j, pl.ds(pl.multiple_of(me * block, 16), block), :], True)
        spectra_part(j, 1, half)

    def spectra_part(j, lo, hi):
        @pl.loop(lo, hi)
        def _(k):
            tile_copy(j, k).wait_recv()
            source = lax.rem(me + n - k, n)
            transform(j, source, landed[j, source], False)

    def whiten(segs):
        for s in segs:
            value = spec[s]
            energy = 2.0 * jnp.mean(value * value, axis=-1, keepdims=True)
            white = (value * lax.rsqrt(energy + 1e-06)).astype(jnp.bfloat16)
            for t in range(PARTS):
                own[s, t] = white[:, t * 128:(t + 1) * 128]
            turn_rows(rows, mid, s, white.astype(jnp.float32))

    odd = lax.rem(me, 2) == 1
    senders = (me >= 1, jnp.logical_and(odd, me >= 2), jnp.logical_and(odd, me + 1 < n))

    def pass_copy(stage, segs, kind):
        part = pl.ds(segs[0], len(segs))
        source, place, back = ((own, near, 1), (own, far, 2), (near, far, 1))[kind]
        return pltpu.make_async_remote_copy(
            src_ref=source.at[part], dst_ref=place.at[part], send_sem=pass_send.at[stage, kind],
            recv_sem=pass_recv.at[stage, min(kind, 1)], device_id={"row": ahead(n - back)}, device_id_type=MESH,
        )

    def pass_start(stage, segs):
        for kind in range(2):
            @pl.when(senders[kind])
            def _():
                pass_copy(stage, segs, kind).start()

    def pass_near(stage, segs):
        @pl.when(me + 1 < n)
        def _():
            pass_copy(stage, segs, 0).wait_recv()

        @pl.when(senders[2])
        def _():
            pass_copy(stage, segs, 2).start()

    def pass_far(stage, segs):
        @pl.when(me + 2 < n)
        def _():
            pass_copy(stage, segs, 1).wait_recv()

    def pass_sent(stage, segs):
        for kind, sends in enumerate(senders):
            @pl.when(sends)
            def _():
                pass_copy(stage, segs, kind).wait_send()

    for i, place in enumerate((near, far)):
        @pl.when(me + i + 1 >= n)
        def _():
            place[...] = jnp.zeros_like(place)

    pairs = GROUP // 2

    def take_rows(parts):
        for slot, source in enumerate((own, near, far)):
            for at, (s, t) in enumerate(parts):
                right[at, slot * block:(slot + 1) * block] = masked(source, s, t, counts, slot)

    def correlate_rows(parts, total, lo, hi):
        @pl.loop(lo // GROUP, hi // GROUP)
        def _(g):
            base = pl.multiple_of(g * GROUP, GROUP)
            for p in range(pairs):
                result = lag_dot(right, turned_pair(rows, mid, lag, parts, base, 2 * p), len(parts))
                for k in range(2):
                    a = base + 2 * p + k
                    for slot in range(SLOTS):
                        part = result[slot * block:(slot + 1) * block, k * LAGS:(k + 1) * LAGS]
                        acc[slot, a] = acc[slot, a] + part if total else part

    last = len(stages) - 1
    middle = block // 2 // GROUP * GROUP
    if not last:
        acc[...] = jnp.zeros_like(acc)

    def spectra(j):
        spectra_first(j)
        spectra_part(j, half, n)

    def arrive(stage):
        segs = stages[stage][1]
        pass_near(stage, segs)
        pass_far(stage, segs)

    for stage, (j, segs, parts) in enumerate(stages):
        for i in range(stages[stage - 1][0] + 1 if stage else 0, j + 1):
            spectra(i)
        whiten(segs)
        pass_start(stage, segs)
        send_next(j)
        if 0 < stage:
            arrive(stage - 1)
            take_rows(stages[stage - 1][2])
            correlate_rows(stages[stage - 1][2], stage > 1, 0, middle)
            if stage == last:
                pass_near(stage, segs)
            correlate_rows(stages[stage - 1][2], stage > 1, middle, block)
    if not last:
        pass_near(last, stages[last][1])
    for j in range(tiles):
        @pl.loop(1, n)
        def _(k):
            tile_copy(j, k).wait_send()
    pass_far(last, stages[last][1])
    for stage, (_, segs, _) in enumerate(stages):
        pass_sent(stage, segs)


def exchange(raw_samples, counts, width, pieces, stages):
    n = lax.axis_size("row")
    segments, local, channels = raw_samples.shape
    block = channels // n
    tiles = len(pieces)
    parts = max(len(parts) for _, _, parts in stages)
    white = jax.ShapeDtypeStruct((segments, PARTS, block, 128), jnp.bfloat16)
    vmem = pl.BlockSpec(memory_space=pltpu.VMEM)
    hbm = pl.BlockSpec(memory_space=pltpu.HBM)
    inputs = (raw_samples.reshape(tiles, width, channels), forward_table().reshape(n, local, WIDTH), lag_tables(), counts)
    return pl.pallas_call(
        functools.partial(exchange_kernel, n, width, pieces, stages),
        out_shape=(white,) * 3 + (jax.ShapeDtypeStruct((SLOTS, block, block, LAGS), jnp.float32),),
        in_specs=[hbm] * 4,
        out_specs=(vmem,) * 4,
        scratch_shapes=[
            pltpu.VMEM((tiles, width, channels), jnp.bfloat16),
            pltpu.VMEM((n, local, WIDTH), jnp.bfloat16),
            pltpu.VMEM((4, LAGS, 128), jnp.bfloat16),
            pltpu.SMEM((1, SLOTS), jnp.int32),
            pltpu.VMEM((tiles, channels, width), jnp.bfloat16),
            pltpu.VMEM((tiles, n, block, width), jnp.bfloat16),
            pltpu.VMEM((segments, block, WIDTH), jnp.float32),
            pltpu.VMEM((parts, SLOTS * block, 128), jnp.bfloat16),
            pltpu.VMEM((segments, PARTS, block, 128), jnp.float32),
            pltpu.VMEM((segments, block, 128), jnp.float32),
            pltpu.SemaphoreType.DMA((tiles + 3,)),
            pltpu.SemaphoreType.DMA((tiles, n)),
            pltpu.SemaphoreType.DMA((tiles, n)),
            pltpu.SemaphoreType.DMA((len(stages), 3)),
            pltpu.SemaphoreType.DMA((len(stages), 2)),
        ],
        compiler_params=pltpu.CompilerParams(collective_id=0, has_side_effects=True, vmem_limit_bytes=20_000_000),
        cost_estimate=pl.CostEstimate(flops=20_000_000_000, bytes_accessed=4_000_000, transcendentals=0),
        name="exchange",
    )(*(pltpu.with_memory_space_constraint(x, pltpu.HBM) for x in inputs))


def correlate_kernel(parts, partner, counts, own, near, far, acc, lag_in, out, right, rows, mid, lag):
    block = own.shape[2]
    step = pl.program_id(0)
    first = pl.multiple_of(step * ROWS_PER_STEP, ROWS_PER_STEP)

    @pl.when(step == 0)
    def _():
        for slot, source in enumerate((own, near, far)):
            for at, (s, t) in enumerate(parts):
                right[at, slot * block:(slot + 1) * block] = masked(source, s, t, counts, slot)
        for s in sorted({s for s, _ in parts}):
            turn_rows(rows, mid, s, jnp.concatenate([own[s, t].astype(jnp.float32) for t in range(PARTS)], axis=1))
        lag[...] = lag_in[...]

    scales = [slot_scale(partner, counts, slot) for slot in range(SLOTS)]
    pairs = ROWS_PER_STEP // 2
    for pair in range(pairs):
        base = pl.multiple_of(first + 2 * pair // GROUP * GROUP, GROUP)
        result = lag_dot(right, turned_pair(rows, mid, lag, parts, base, 2 * pair % GROUP), len(parts))
        for k in range(2):
            i = 2 * pair + k
            a = first + i
            for slot in range(SLOTS):
                part = result[slot * block:(slot + 1) * block, k * LAGS:(k + 1) * LAGS]
                part = (acc[slot, a] + part) * scales[slot]
                if slot == 0:
                    part = jnp.where(lax.broadcasted_iota(jnp.int32, part.shape, 0) > a, part, 0.0)
                out[0, slot, i] = part.astype(jnp.bfloat16)


def correlate(parts, partner, counts, own, near, far, acc):
    segments, _, block, _ = own.shape
    vmem = pl.BlockSpec(memory_space=pltpu.VMEM)
    return pl.pallas_call(
        functools.partial(correlate_kernel, parts),
        grid_spec=pltpu.PrefetchScalarGridSpec(
            num_scalar_prefetch=0,
            grid=(block // ROWS_PER_STEP,),
            in_specs=[pl.BlockSpec(memory_space=pltpu.SMEM)] * 2 + [vmem] * 5,
            out_specs=pl.BlockSpec((1, SLOTS, ROWS_PER_STEP, block, LAGS), lambda i, *_: (0, 0, i, 0, 0)),
            scratch_shapes=[
                pltpu.VMEM((len(parts), SLOTS * block, 128), jnp.bfloat16),
                pltpu.VMEM((segments, PARTS, block, 128), jnp.float32),
                pltpu.VMEM((segments, block, 128), jnp.float32),
                pltpu.VMEM((4, LAGS, 128), jnp.bfloat16),
            ],
        ),
        out_shape=jax.ShapeDtypeStruct((1, SLOTS, block, block, LAGS), jnp.bfloat16),
        cost_estimate=pl.CostEstimate(
            flops=6 * block * block * LAGS * len(parts) * 128, bytes_accessed=6_000_000, transcendentals=0),
        compiler_params=pltpu.CompilerParams(vmem_limit_bytes=10 * 2**20),
        name="correlate",
    )(partner, counts, own, near, far, acc, lag_tables())


def on_device(raw_samples, partner, counts):
    width, pieces, stages = tile_plan(raw_samples.shape[0], raw_samples.shape[1])
    own, near, far, acc = exchange(raw_samples, counts, width, pieces, stages)
    return correlate(stages[-1][2], partner, counts, own, near, far, acc)


def solution(mesh):
    return jax.shard_map(
        on_device,
        mesh=mesh,
        in_specs=(P("groups", "row", None), P(("groups", "row"), None), P(("groups", "row"), None)),
        out_specs=P(("groups", "row"), None, None, None, None),
        check_vma=False,
    )
```

time: 54.3 us -> 47.4 us (0.87)
  the two profiles are of different devices: /device:TPU:24 before, /device:TPU:1 now
where the time goes in v1:
time: 47.4 us; the launch traced here: 47.3 us
  Pallas kernels  47.2 us (100%)
    pallas_call x1, Pallas kernels, exchange(): pl.pallas_call(functools.partial(exchange_kernel, n, width, pieces, stage...  39.8 us
    pallas_call x1, Pallas kernels, correlate(): pl.pallas_call(functools.partial(correlate_kernel, parts), grid_spec=pltp...  7.45 us

profile of v1, /device:TPU:1, one launch (start us, length us, event | category | flops | bytes accessed | tf_op | source)
XLA Modules:
  0.0 47.3 jit_solution(18057148215614284619)
XLA Ops:
  0.0 0.0 copy-start
  0.0 0.0 copy-start.1
  0.0 0.0 copy-start.2
  0.0 39.8 %exchange.1 = (bf16[4,3,80,128]{3,2,1,0:T(8,128)(2,1)S(1)}, bf16[4,3,80,128]{3,2,1,0:T(8,128)(2,1)S(1)}, bf16[4,3,80,128]{3,2,1,0:T(8,128)(2,1)S(1)}, f32[3,80,80,128]{3,2,1,0:T(8,128)S(1)}) custom-call(bf16[3,128,1280]{2,1,0:T(8,128)(2,1)} %bitcast.1, bf16[16,96,384]{2,1,0:T(8,128)(2,1)} %constant.9.table_hbm, ...), custom_call_target="tpu_custom_call" | custom-call | flops 20000000000 | bytes 4000000 | tf_op jit(solution)/shard_map/exchange/pallas_call | solution.py:309
  39.8 0.0 copy-done
  39.8 0.0 copy-done.1
  39.8 0.0 copy-done.2
  39.8 7.5 %correlate.1 = bf16[1,3,80,80,128]{4,3,2,1,0:T(8,128)(2,1)} custom-call(s32[1,3]{1,0:T(1,128)S(1)} %copy-done.1, s32[1,3]{1,0:T(1,128)S(1)} %copy-done.2, bf16[4,3,80,128]{3,2,1,0:T(8,128)(2,1)S(1)} %get-tuple-element.9.own, bf16[4,3,80,128]{3,2,1,0:T(8,128)(2,1)S(1)} %get-tuple-element.10.near, bf16[4,3,80,128]{3,2,1,0:T(8,128)(2,1)S(1)} %get-tuple-element.11.far, ...), custom_call_target="tpu_custom_call" | custom-call | flops 3774873600 | bytes 6000000 | tf_op jit(solution)/shard_map/correlate/pallas_call | solution.py:370
Async XLA Ops:
  0.0 39.8 %copy-start = (bf16[4,128,128]{2,1,0:T(8,128)(2,1)S(1)}, bf16[4,128,128]{2,1,0:T(8,128)(2,1)}, u32[]{:S(2)}) copy-start(bf16[4,128,128]{2,1,0:T(8,128)(2,1)} %constant.10.lag_hbm.lag_in) | copy-start | bytes 393220
  0.0 39.8 %copy-start.1 = (s32[1,3]{1,0:T(1,128)S(1)}, s32[1,3]{1,0:T(1,128)}, u32[]{:S(2)}) copy-start(s32[1,3]{1,0:T(1,128)} %partner.1) | copy-start | bytes 40
  0.0 39.8 %copy-start.2 = (s32[1,3]{1,0:T(1,128)S(1)}, s32[1,3]{1,0:T(1,128)}, u32[]{:S(2)}) copy-start(s32[1,3]{1,0:T(1,128)} %counts.1) | copy-start | bytes 40

commit v2 on v1

--- a/solution.py
+++ b/solution.py
@@ -19,7 +19,7 @@
 HALF = BINS - 128
 PARTS = WIDTH // 128
 GROUP = 8
-ROWS_PER_STEP = 16
+RUN = 40
 MESH = pl.DeviceIdType.MESH
 
 
@@ -239,7 +239,6 @@
         def _():
             place[...] = jnp.zeros_like(place)
 
-    pairs = GROUP // 2
 
     def take_rows(parts):
         for slot, source in enumerate((own, near, far)):
@@ -247,19 +246,19 @@
                 right[at, slot * block:(slot + 1) * block] = masked(source, s, t, counts, slot)
 
     def correlate_rows(parts, total, lo, hi):
-        @pl.loop(lo // GROUP, hi // GROUP)
+        @pl.loop(0, (hi - lo) // RUN)
         def _(g):
-            base = pl.multiple_of(g * GROUP, GROUP)
-            for p in range(pairs):
-                result = lag_dot(right, turned_pair(rows, mid, lag, parts, base, 2 * p), len(parts))
+            base = pl.multiple_of(lo + g * RUN, GROUP)
+            for i in range(0, RUN, 2):
+                result = lag_dot(right, turned_pair(rows, mid, lag, parts, base + i // GROUP * GROUP, i % GROUP), len(parts))
                 for k in range(2):
-                    a = base + 2 * p + k
+                    a = base + i + k
                     for slot in range(SLOTS):
                         part = result[slot * block:(slot + 1) * block, k * LAGS:(k + 1) * LAGS]
                         acc[slot, a] = acc[slot, a] + part if total else part
 
     last = len(stages) - 1
-    middle = block // 2 // GROUP * GROUP
+    middle = block // 2 // RUN * RUN
     if not last:
         acc[...] = jnp.zeros_like(acc)
 
@@ -334,34 +333,33 @@
     )(*(pltpu.with_memory_space_constraint(x, pltpu.HBM) for x in inputs))
 
 
-def correlate_kernel(parts, partner, counts, own, near, far, acc, lag_in, out, right, rows, mid, lag):
+def correlate_kernel(parts, partner, counts, own, near, far, acc, lag_in, out, staged, right, rows, mid, lag, out_sem):
     block = own.shape[2]
-    step = pl.program_id(0)
-    first = pl.multiple_of(step * ROWS_PER_STEP, ROWS_PER_STEP)
-
-    @pl.when(step == 0)
-    def _():
-        for slot, source in enumerate((own, near, far)):
-            for at, (s, t) in enumerate(parts):
-                right[at, slot * block:(slot + 1) * block] = masked(source, s, t, counts, slot)
-        for s in sorted({s for s, _ in parts}):
-            turn_rows(rows, mid, s, jnp.concatenate([own[s, t].astype(jnp.float32) for t in range(PARTS)], axis=1))
-        lag[...] = lag_in[...]
-
+    for slot, source in enumerate((own, near, far)):
+        for at, (s, t) in enumerate(parts):
+            right[at, slot * block:(slot + 1) * block] = masked(source, s, t, counts, slot)
+    for s in sorted({s for s, _ in parts}):
+        turn_rows(rows, mid, s, jnp.concatenate([own[s, t].astype(jnp.float32) for t in range(PARTS)], axis=1))
+    lag[...] = lag_in[...]
     scales = [slot_scale(partner, counts, slot) for slot in range(SLOTS)]
-    pairs = ROWS_PER_STEP // 2
-    for pair in range(pairs):
-        base = pl.multiple_of(first + 2 * pair // GROUP * GROUP, GROUP)
-        result = lag_dot(right, turned_pair(rows, mid, lag, parts, base, 2 * pair % GROUP), len(parts))
+
+    def write(g):
+        here = pl.ds(g * GROUP, GROUP)
+        return pltpu.make_async_copy(staged.at[:, here], out.at[0, :, here], out_sem.at[g])
+
+    for a in range(0, block, 2):
+        result = lag_dot(right, turned_pair(rows, mid, lag, parts, a // GROUP * GROUP, a % GROUP), len(parts))
         for k in range(2):
-            i = 2 * pair + k
-            a = first + i
             for slot in range(SLOTS):
                 part = result[slot * block:(slot + 1) * block, k * LAGS:(k + 1) * LAGS]
-                part = (acc[slot, a] + part) * scales[slot]
+                part = (acc[slot, a + k] + part) * scales[slot]
                 if slot == 0:
-                    part = jnp.where(lax.broadcasted_iota(jnp.int32, part.shape, 0) > a, part, 0.0)
-                out[0, slot, i] = part.astype(jnp.bfloat16)
+                    part = jnp.where(lax.broadcasted_iota(jnp.int32, part.shape, 0) > a + k, part, 0.0)
+                staged[slot, a + k] = part.astype(jnp.bfloat16)
+        if (a + 2) % GROUP == 0:
+            write(a // GROUP).start()
+    for g in range(block // GROUP):
+        write(g).wait()
 
 
 def correlate(parts, partner, counts, own, near, far, acc):
@@ -369,22 +367,20 @@
     vmem = pl.BlockSpec(memory_space=pltpu.VMEM)
     return pl.pallas_call(
         functools.partial(correlate_kernel, parts),
-        grid_spec=pltpu.PrefetchScalarGridSpec(
-            num_scalar_prefetch=0,
-            grid=(block // ROWS_PER_STEP,),
-            in_specs=[pl.BlockSpec(memory_space=pltpu.SMEM)] * 2 + [vmem] * 5,
-            out_specs=pl.BlockSpec((1, SLOTS, ROWS_PER_STEP, block, LAGS), lambda i, *_: (0, 0, i, 0, 0)),
-            scratch_shapes=[
-                pltpu.VMEM((len(parts), SLOTS * block, 128), jnp.bfloat16),
-                pltpu.VMEM((segments, PARTS, block, 128), jnp.float32),
-                pltpu.VMEM((segments, block, 128), jnp.float32),
-                pltpu.VMEM((4, LAGS, 128), jnp.bfloat16),
-            ],
-        ),
+        in_specs=[pl.BlockSpec(memory_space=pltpu.SMEM)] * 2 + [vmem] * 5,
+        out_specs=pl.BlockSpec(memory_space=pltpu.HBM),
+        scratch_shapes=[
+            pltpu.VMEM((SLOTS, block, block, LAGS), jnp.bfloat16),
+            pltpu.VMEM((len(parts), SLOTS * block, 128), jnp.bfloat16),
+            pltpu.VMEM((segments, PARTS, block, 128), jnp.float32),
+            pltpu.VMEM((segments, block, 128), jnp.float32),
+            pltpu.VMEM((4, LAGS, 128), jnp.bfloat16),
+            pltpu.SemaphoreType.DMA((block // GROUP,)),
+        ],
         out_shape=jax.ShapeDtypeStruct((1, SLOTS, block, block, LAGS), jnp.bfloat16),
         cost_estimate=pl.CostEstimate(
             flops=6 * block * block * LAGS * len(parts) * 128, bytes_accessed=6_000_000, transcendentals=0),
-        compiler_params=pltpu.CompilerParams(vmem_limit_bytes=10 * 2**20),
+        compiler_params=pltpu.CompilerParams(vmem_limit_bytes=15 * 2**20),
         name="correlate",
     )(partner, counts, own, near, far, acc, lag_tables())
 

time: 47.4 us -> 45.2 us (0.954)
  the two profiles are of different devices: /device:TPU:1 before, /device:TPU:0 now
where the time goes in v2:
time: 45.2 us; the launch traced here: 44.4 us
  Pallas kernels  44.3 us (98%)
    pallas_call x1, Pallas kernels, exchange(): pl.pallas_call(functools.partial(exchange_kernel, n, width, pieces, stage...  38.2 us
    pallas_call x1, Pallas kernels, correlate(): pl.pallas_call(functools.partial(correlate_kernel, parts), in_specs=[pl.B...  6.11 us

profile of v2, /device:TPU:0, one launch (start us, length us, event | category | flops | bytes accessed | tf_op | source)
XLA Modules:
  0.0 44.4 jit_solution(652970217581890348)
XLA Ops:
  0.0 0.0 copy-start
  0.0 0.0 copy-start.1
  0.0 0.0 copy-start.2
  0.0 38.2 %exchange.1 = (bf16[4,3,80,128]{3,2,1,0:T(8,128)(2,1)S(1)}, bf16[4,3,80,128]{3,2,1,0:T(8,128)(2,1)S(1)}, bf16[4,3,80,128]{3,2,1,0:T(8,128)(2,1)S(1)}, f32[3,80,80,128]{3,2,1,0:T(8,128)S(1)}) custom-call(bf16[3,128,1280]{2,1,0:T(8,128)(2,1)} %bitcast.1, bf16[16,96,384]{2,1,0:T(8,128)(2,1)} %constant.9.table_hbm, ...), custom_call_target="tpu_custom_call" | custom-call | flops 20000000000 | bytes 4000000 | tf_op jit(solution)/shard_map/exchange/pallas_call | solution.py:308
  38.2 0.0 copy-done
  38.2 0.0 copy-done.1
  38.3 0.0 copy-done.2
  38.3 6.1 %correlate.1 = bf16[1,3,80,80,128]{4,3,2,1,0:T(8,128)(2,1)} custom-call(s32[1,3]{1,0:T(1,128)S(1)} %copy-done.1, s32[1,3]{1,0:T(1,128)S(1)} %copy-done.2, bf16[4,3,80,128]{3,2,1,0:T(8,128)(2,1)S(1)} %get-tuple-element.9.own, bf16[4,3,80,128]{3,2,1,0:T(8,128)(2,1)S(1)} %get-tuple-element.10.near, bf16[4,3,80,128]{3,2,1,0:T(8,128)(2,1)S(1)} %get-tuple-element.11.far, ...), custom_call_target="tpu_custom_call" | custom-call | flops 3774873600 | bytes 6000000 | tf_op jit(solution)/shard_map/correlate/pallas_call | solution.py:368
Async XLA Ops:
  0.0 38.2 %copy-start = (bf16[4,128,128]{2,1,0:T(8,128)(2,1)S(1)}, bf16[4,128,128]{2,1,0:T(8,128)(2,1)}, u32[]{:S(2)}) copy-start(bf16[4,128,128]{2,1,0:T(8,128)(2,1)} %constant.10.lag_hbm.lag_in) | copy-start | bytes 393220
  0.0 38.2 %copy-start.1 = (s32[1,3]{1,0:T(1,128)S(1)}, s32[1,3]{1,0:T(1,128)}, u32[]{:S(2)}) copy-start(s32[1,3]{1,0:T(1,128)} %partner.1) | copy-start | bytes 40
  0.0 38.3 %copy-start.2 = (s32[1,3]{1,0:T(1,128)S(1)}, s32[1,3]{1,0:T(1,128)}, u32[]{:S(2)}) copy-start(s32[1,3]{1,0:T(1,128)} %counts.1) | copy-start | bytes 40

commit v3 on v2

--- a/solution.py
+++ b/solution.py
@@ -63,7 +63,7 @@
                 row.append((s, lo - j * width, hi - j * width, lo - s * local))
         pieces.append(row)
         whole = (j + 1) * width // local
-        if whole > done:
+        if whole > done and j >= tiles - 2:
             ready = whole * PARTS
             ready -= ready % 2 if j < tiles - 1 else 0
             stages.append((j, list(range(done, whole)), parts[used:ready]))
@@ -166,8 +166,7 @@
 
         if j == 0:
             pl.semaphore_wait(barrier, n - 1)
-        if j < 2:
-            send(j, 1, n)
+        send(j, 1, n)
 
     for copy in more:
         copy.wait()
@@ -276,7 +275,6 @@
             spectra(i)
         whiten(segs)
         pass_start(stage, segs)
-        send_next(j)
         if 0 < stage:
             arrive(stage - 1)
             take_rows(stages[stage - 1][2])

time: 45.2 us -> 42.8 us (0.947); the launches traced: 44.4 us -> 42.7 us
  Pallas kernels: 44.3 us -> 42.6 us
    pallas_call x1, Pallas kernels: 38.2 us -> 36.5 us  [exchange(): pl.pallas_call(functools.partial(exchange_kernel, n, width, pieces, stage...]
where the time goes in v3:
time: 42.8 us; the launch traced here: 42.7 us
  Pallas kernels  42.6 us (100%)
    pallas_call x1, Pallas kernels, exchange(): pl.pallas_call(functools.partial(exchange_kernel, n, width, pieces, stage...  36.5 us
    pallas_call x1, Pallas kernels, correlate(): pl.pallas_call(functools.partial(correlate_kernel, parts), in_specs=[pl.B...  6.11 us

profile of v3, /device:TPU:0, one launch (start us, length us, event | category | flops | bytes accessed | tf_op | source)
XLA Modules:
  0.0 42.7 jit_solution(13996031549234370645)
XLA Ops:
  0.0 0.0 copy-start
  0.0 0.0 copy-start.1
  0.0 0.0 copy-start.2
  0.0 36.5 %exchange.1 = (bf16[4,3,80,128]{3,2,1,0:T(8,128)(2,1)S(1)}, bf16[4,3,80,128]{3,2,1,0:T(8,128)(2,1)S(1)}, bf16[4,3,80,128]{3,2,1,0:T(8,128)(2,1)S(1)}, f32[3,80,80,128]{3,2,1,0:T(8,128)S(1)}) custom-call(bf16[3,128,1280]{2,1,0:T(8,128)(2,1)} %bitcast.1, bf16[16,96,384]{2,1,0:T(8,128)(2,1)} %constant.9.table_hbm, ...), custom_call_target="tpu_custom_call" | custom-call | flops 20000000000 | bytes 4000000 | tf_op jit(solution)/shard_map/exchange/pallas_call | solution.py:306
  36.5 0.0 copy-done
  36.5 0.0 copy-done.1
  36.6 0.0 copy-done.2
  36.6 6.1 %correlate.1 = bf16[1,3,80,80,128]{4,3,2,1,0:T(8,128)(2,1)} custom-call(s32[1,3]{1,0:T(1,128)S(1)} %copy-done.1, s32[1,3]{1,0:T(1,128)S(1)} %copy-done.2, bf16[4,3,80,128]{3,2,1,0:T(8,128)(2,1)S(1)} %get-tuple-element.9.own, bf16[4,3,80,128]{3,2,1,0:T(8,128)(2,1)S(1)} %get-tuple-element.10.near, bf16[4,3,80,128]{3,2,1,0:T(8,128)(2,1)S(1)} %get-tuple-element.11.far, ...), custom_call_target="tpu_custom_call" | custom-call | flops 3774873600 | bytes 6000000 | tf_op jit(solution)/shard_map/correlate/pallas_call | solution.py:366
Async XLA Ops:
  0.0 36.5 %copy-start = (bf16[4,128,128]{2,1,0:T(8,128)(2,1)S(1)}, bf16[4,128,128]{2,1,0:T(8,128)(2,1)}, u32[]{:S(2)}) copy-start(bf16[4,128,128]{2,1,0:T(8,128)(2,1)} %constant.10.lag_hbm.lag_in) | copy-start | bytes 393220
  0.0 36.5 %copy-start.1 = (s32[1,3]{1,0:T(1,128)S(1)}, s32[1,3]{1,0:T(1,128)}, u32[]{:S(2)}) copy-start(s32[1,3]{1,0:T(1,128)} %partner.1) | copy-start | bytes 40
  0.0 36.6 %copy-start.2 = (s32[1,3]{1,0:T(1,128)S(1)}, s32[1,3]{1,0:T(1,128)}, u32[]{:S(2)}) copy-start(s32[1,3]{1,0:T(1,128)} %counts.1) | copy-start | bytes 40

commit v4 on v3

--- a/solution.py
+++ b/solution.py
@@ -19,7 +19,6 @@
 HALF = BINS - 128
 PARTS = WIDTH // 128
 GROUP = 8
-RUN = 40
 MESH = pl.DeviceIdType.MESH
 
 
@@ -245,19 +244,15 @@
                 right[at, slot * block:(slot + 1) * block] = masked(source, s, t, counts, slot)
 
     def correlate_rows(parts, total, lo, hi):
-        @pl.loop(0, (hi - lo) // RUN)
-        def _(g):
-            base = pl.multiple_of(lo + g * RUN, GROUP)
-            for i in range(0, RUN, 2):
-                result = lag_dot(right, turned_pair(rows, mid, lag, parts, base + i // GROUP * GROUP, i % GROUP), len(parts))
-                for k in range(2):
-                    a = base + i + k
-                    for slot in range(SLOTS):
-                        part = result[slot * block:(slot + 1) * block, k * LAGS:(k + 1) * LAGS]
-                        acc[slot, a] = acc[slot, a] + part if total else part
+        for a in range(lo, hi, 2):
+            result = lag_dot(right, turned_pair(rows, mid, lag, parts, a // GROUP * GROUP, a % GROUP), len(parts))
+            for k in range(2):
+                for slot in range(SLOTS):
+                    part = result[slot * block:(slot + 1) * block, k * LAGS:(k + 1) * LAGS]
+                    acc[slot, a + k] = acc[slot, a + k] + part if total else part
 
     last = len(stages) - 1
-    middle = block // 2 // RUN * RUN
+    middle = block * 8 // 10 // GROUP * GROUP
     if not last:
         acc[...] = jnp.zeros_like(acc)
 

time: 42.8 us -> 42.8 us (level)
  no operation moved by 1% of the time
where the time goes in v4:
time: 42.8 us; the launch traced here: 42.7 us
  Pallas kernels  42.6 us (100%)
    pallas_call x1, Pallas kernels, exchange(): pl.pallas_call(functools.partial(exchange_kernel, n, width, pieces, stage...  36.5 us
    pallas_call x1, Pallas kernels, correlate(): pl.pallas_call(functools.partial(correlate_kernel, parts), in_specs=[pl.B...  6.11 us

profile of v4, /device:TPU:0, one launch (start us, length us, event | category | flops | bytes accessed | tf_op | source)
XLA Modules:
  0.0 42.7 jit_solution(13163655351846735768)
XLA Ops:
  0.0 0.0 copy-start
  0.0 0.0 copy-start.1
  0.0 0.0 copy-start.2
  0.0 36.5 %exchange.1 = (bf16[4,3,80,128]{3,2,1,0:T(8,128)(2,1)S(1)}, bf16[4,3,80,128]{3,2,1,0:T(8,128)(2,1)S(1)}, bf16[4,3,80,128]{3,2,1,0:T(8,128)(2,1)S(1)}, f32[3,80,80,128]{3,2,1,0:T(8,128)S(1)}) custom-call(bf16[3,128,1280]{2,1,0:T(8,128)(2,1)} %bitcast.1, bf16[16,96,384]{2,1,0:T(8,128)(2,1)} %constant.9.table_hbm, ...), custom_call_target="tpu_custom_call" | custom-call | flops 20000000000 | bytes 4000000 | tf_op jit(solution)/shard_map/exchange/pallas_call | solution.py:301
  36.5 0.0 copy-done
  36.5 0.0 copy-done.1
  36.5 0.0 copy-done.2
  36.6 6.1 %correlate.1 = bf16[1,3,80,80,128]{4,3,2,1,0:T(8,128)(2,1)} custom-call(s32[1,3]{1,0:T(1,128)S(1)} %copy-done.1, s32[1,3]{1,0:T(1,128)S(1)} %copy-done.2, bf16[4,3,80,128]{3,2,1,0:T(8,128)(2,1)S(1)} %get-tuple-element.9.own, bf16[4,3,80,128]{3,2,1,0:T(8,128)(2,1)S(1)} %get-tuple-element.10.near, bf16[4,3,80,128]{3,2,1,0:T(8,128)(2,1)S(1)} %get-tuple-element.11.far, ...), custom_call_target="tpu_custom_call" | custom-call | flops 3774873600 | bytes 6000000 | tf_op jit(solution)/shard_map/correlate/pallas_call | solution.py:361
Async XLA Ops:
  0.0 36.5 %copy-start = (bf16[4,128,128]{2,1,0:T(8,128)(2,1)S(1)}, bf16[4,128,128]{2,1,0:T(8,128)(2,1)}, u32[]{:S(2)}) copy-start(bf16[4,128,128]{2,1,0:T(8,128)(2,1)} %constant.10.lag_hbm.lag_in) | copy-start | bytes 393220
  0.0 36.5 %copy-start.1 = (s32[1,3]{1,0:T(1,128)S(1)}, s32[1,3]{1,0:T(1,128)}, u32[]{:S(2)}) copy-start(s32[1,3]{1,0:T(1,128)} %partner.1) | copy-start | bytes 40
  0.0 36.5 %copy-start.2 = (s32[1,3]{1,0:T(1,128)S(1)}, s32[1,3]{1,0:T(1,128)}, u32[]{:S(2)}) copy-start(s32[1,3]{1,0:T(1,128)} %counts.1) | copy-start | bytes 40

commit v5 on v3

--- a/solution.py
+++ b/solution.py
@@ -19,7 +19,7 @@
 HALF = BINS - 128
 PARTS = WIDTH // 128
 GROUP = 8
-RUN = 40
+RUN = 80
 MESH = pl.DeviceIdType.MESH
 
 
@@ -278,10 +278,9 @@
         if 0 < stage:
             arrive(stage - 1)
             take_rows(stages[stage - 1][2])
-            correlate_rows(stages[stage - 1][2], stage > 1, 0, middle)
+            correlate_rows(stages[stage - 1][2], stage > 1, 0, block)
             if stage == last:
                 pass_near(stage, segs)
-            correlate_rows(stages[stage - 1][2], stage > 1, middle, block)
     if not last:
         pass_near(last, stages[last][1])
     for j in range(tiles):

time: 42.8 us -> 42.6 us (level)
  no operation moved by 1% of the time
where the time goes in v5:
time: 42.6 us; the launch traced here: 42.5 us
  Pallas kernels  42.4 us (100%)
    pallas_call x1, Pallas kernels, exchange(): pl.pallas_call(functools.partial(exchange_kernel, n, width, pieces, stage...  36.3 us
    pallas_call x1, Pallas kernels, correlate(): pl.pallas_call(functools.partial(correlate_kernel, parts), in_specs=[pl.B...  6.13 us

profile of v5, /device:TPU:0, one launch (start us, length us, event | category | flops | bytes accessed | tf_op | source)
XLA Modules:
  0.0 42.5 jit_solution(13254464088757528245)
XLA Ops:
  0.0 0.0 copy-start
  0.0 0.0 copy-start.1
  0.0 0.0 copy-start.2
  0.0 36.3 %exchange.1 = (bf16[4,3,80,128]{3,2,1,0:T(8,128)(2,1)S(1)}, bf16[4,3,80,128]{3,2,1,0:T(8,128)(2,1)S(1)}, bf16[4,3,80,128]{3,2,1,0:T(8,128)(2,1)S(1)}, f32[3,80,80,128]{3,2,1,0:T(8,128)S(1)}) custom-call(bf16[3,128,1280]{2,1,0:T(8,128)(2,1)} %bitcast.1, bf16[16,96,384]{2,1,0:T(8,128)(2,1)} %constant.9.table_hbm, ...), custom_call_target="tpu_custom_call" | custom-call | flops 20000000000 | bytes 4000000 | tf_op jit(solution)/shard_map/exchange/pallas_call | solution.py:305
  36.3 0.0 copy-done
  36.3 0.0 copy-done.1
  36.4 0.0 copy-done.2
  36.4 6.1 %correlate.1 = bf16[1,3,80,80,128]{4,3,2,1,0:T(8,128)(2,1)} custom-call(s32[1,3]{1,0:T(1,128)S(1)} %copy-done.1, s32[1,3]{1,0:T(1,128)S(1)} %copy-done.2, bf16[4,3,80,128]{3,2,1,0:T(8,128)(2,1)S(1)} %get-tuple-element.9.own, bf16[4,3,80,128]{3,2,1,0:T(8,128)(2,1)S(1)} %get-tuple-element.10.near, bf16[4,3,80,128]{3,2,1,0:T(8,128)(2,1)S(1)} %get-tuple-element.11.far, ...), custom_call_target="tpu_custom_call" | custom-call | flops 3774873600 | bytes 6000000 | tf_op jit(solution)/shard_map/correlate/pallas_call | solution.py:365
Async XLA Ops:
  0.0 36.3 %copy-start = (bf16[4,128,128]{2,1,0:T(8,128)(2,1)S(1)}, bf16[4,128,128]{2,1,0:T(8,128)(2,1)}, u32[]{:S(2)}) copy-start(bf16[4,128,128]{2,1,0:T(8,128)(2,1)} %constant.10.lag_hbm.lag_in) | copy-start | bytes 393220
  0.0 36.3 %copy-start.1 = (s32[1,3]{1,0:T(1,128)S(1)}, s32[1,3]{1,0:T(1,128)}, u32[]{:S(2)}) copy-start(s32[1,3]{1,0:T(1,128)} %partner.1) | copy-start | bytes 40
  0.0 36.3 %copy-start.2 = (s32[1,3]{1,0:T(1,128)S(1)}, s32[1,3]{1,0:T(1,128)}, u32[]{:S(2)}) copy-start(s32[1,3]{1,0:T(1,128)} %counts.1) | copy-start | bytes 40
